TPU v7x, 32 devices: a whole 2x2x4 slice. The times are simulated.
32 devices in a mesh: node: 4 (over z), local: 8 (over y, x, core).
Axes of the slice: x: 2, y: 2, z: 4, core: 2. Of those that a mesh axis runs over, the one named last changes fastest.
Arguments:
- tokens: bfloat16 [4096, 5120], P(('node', 'local')), may hold values from -6 to 6
- routes: int32 [4096, 6], P(('node', 'local')), may hold values from 0 to 31, all different within a row; in each aligned block of 128 rows (0 to 127, 128 to 255, ...) at most 32 rows name the same one
- route_weights: float32 [4096, 6], P(('node', 'local')), may hold values from 0.05 to 1
- w_gate: bfloat16 [32, 5120, 768], P(('node', 'local')), may hold values from -0.078125 to 0.078125
- w_up: bfloat16 [32, 5120, 768], P(('node', 'local')), may hold values from -0.078125 to 0.078125
- w_down: bfloat16 [32, 768, 5120], P(('node', 'local')), may hold values from -0.21875 to 0.21875
Outputs:
- mixed: bfloat16 [4096, 5120], P(('node', 'local'))
- balance_loss: float32 [], replicated
Inputs may be any that keep to these rules, and one draw needn't show every extreme that they name: `routes`: each row names 6 different experts. Among the rows of one device no expert is named more than 32 times, a bound that some block reaches.
All inputs are finite; a program needn't handle non-finite values.
Results may differ from a plain program's by a relative error of at most 0.0025.
The roundings to bfloat16 on the way count: a program that leaves them out, or rounds other values in their place, can miss the bound.
Values may be sent and summed in bfloat16 or wider, within the bound.
A program may use at most 128 MiB of HBM per device.

v0:
```python
import functools

import jax
import jax.numpy as jnp
from jax import lax
from jax.experimental import pallas as pl
from jax.experimental.pallas import tpu as pltpu
from jax.sharding import PartitionSpec as P

MESH = pl.DeviceIdType.MESH
VMEM_LIMIT = 62 * 1024 * 1024


def chunks_of(width):
    return max(n for n in range(1, 11) if width % (n * 128) == 0)


def greet(nn, nl, mn, ml):
    barrier = pltpu.get_barrier_semaphore()
    for k in range(1, nn):
        pl.semaphore_signal(barrier, inc=1, device_id={"node": lax.rem(mn + k, nn)}, device_id_type=MESH)
    for k in range(1, nl):
        pl.semaphore_signal(barrier, inc=1, device_id={"local": lax.rem(ml + k, nl)}, device_id_type=MESH)
    pl.semaphore_wait(barrier, nn + nl - 2)


def dispatch_kernel(nn, nl, nch, tok, pick, out, held, sent, z_send, z_recv, p_send, p_recv, own_sem):
    mn, ml = lax.axis_index("node"), lax.axis_index("local")
    tok_dev, width = tok.shape
    ch = width // nch
    rows = out.shape[1]
    mine = pl.ds(pl.multiple_of(mn * tok_dev, tok_dev), tok_dev)

    def cols(c):
        return pl.ds(pl.multiple_of(c * ch, 128), ch)

    def along(c, k):
        return pltpu.make_async_remote_copy(
            src_ref=tok.at[:, cols(c)],
            dst_ref=held.at[c, mine, :],
            send_sem=z_send.at[c, k - 1],
            recv_sem=z_recv.at[c, k - 1],
            device_id={"node": lax.rem(mn + k, nn)},
            device_id_type=MESH,
        )

    def block(e):
        return pl.ds(pl.multiple_of(e * rows, rows), rows)

    def within(c, k):
        e = lax.rem(ml + k, nl)
        return pltpu.make_async_remote_copy(
            src_ref=sent.at[c, block(e), :],
            dst_ref=out.at[ml, :, cols(c)],
            send_sem=p_send.at[c, k - 1],
            recv_sem=p_recv.at[c, k - 1],
            device_id={"local": e},
            device_id_type=MESH,
        )

    def own(c):
        return pltpu.make_async_copy(sent.at[c, block(ml), :], out.at[ml, :, cols(c)], own_sem.at[c])

    greet(nn, nl, mn, ml)

    @pl.loop(0, nch)
    def _(c):
        for k in range(1, nn):
            along(c, k).start()

    @pl.loop(0, nch)
    def _(c):
        held[c, mine, :] = tok[:, cols(c)]

    @pl.loop(0, nch)
    def _(c):
        for k in range(1, nn):
            along(c, k).wait_recv()
        picked = jnp.dot(pick[...], held[c], preferred_element_type=jnp.float32)
        sent[c] = picked.astype(jnp.bfloat16)
        for k in range(1, nl):
            within(c, k).start()
        own(c).start()

    @pl.loop(0, nch)
    def _(c):
        for k in range(1, nl):
            within(c, k).wait_recv()
        own(c).wait()
        for k in range(1, nn):
            along(c, k).wait_send()
        for k in range(1, nl):
            within(c, k).wait_send()


def return_kernel(nn, nl, nch, y, mix, out, held, part, got, p_send, p_recv, z_send, z_recv, own_sem):
    mn, ml = lax.axis_index("node"), lax.axis_index("local")
    tok_dev, width = out.shape
    ch = width // nch
    rows = y.shape[1]
    lines = nn * tok_dev
    mine = pl.ds(pl.multiple_of(ml * rows, rows), rows)

    def cols(c):
        return pl.ds(pl.multiple_of(c * ch, 128), ch)

    def within(c, k):
        e = lax.rem(ml + k, nl)
        return pltpu.make_async_remote_copy(
            src_ref=y.at[e, :, cols(c)],
            dst_ref=held.at[c, mine, :],
            send_sem=p_send.at[c, k - 1],
            recv_sem=p_recv.at[c, k - 1],
            device_id={"local": e},
            device_id_type=MESH,
        )

    def own(c):
        return pltpu.make_async_copy(y.at[ml, :, cols(c)], held.at[c, mine, :], own_sem.at[c])

    def tokens_of(p):
        return pl.ds(pl.multiple_of(p * tok_dev, tok_dev), tok_dev)

    def along(c, k):
        p = lax.rem(mn + k, nn)
        return pltpu.make_async_remote_copy(
            src_ref=part.at[c, tokens_of(p), :],
            dst_ref=got.at[c, k - 1],
            send_sem=z_send.at[c, k - 1],
            recv_sem=z_recv.at[c, k - 1],
            device_id={"node": p},
            device_id_type=MESH,
        )

    greet(nn, nl, mn, ml)

    @pl.loop(0, nch)
    def _(c):
        for k in range(1, nl):
            within(c, k).start()
        own(c).start()

    @pl.loop(0, nch)
    def _(c):
        for k in range(1, nl):
            within(c, k).wait_recv()
        own(c).wait()
        terms = [
            jnp.dot(mix[pl.ds(i * lines, lines), :], held[c], preferred_element_type=jnp.float32)
            for i in range(3)
        ]
        part[c] = terms[0] + terms[1] + terms[2]
        for k in range(1, nn):
            along(c, k).start()

    @pl.loop(0, nch)
    def _(c):
        total = part[c, tokens_of(mn), :]
        for k in range(1, nn):
            along(c, k).wait_recv()
        for k in range(1, nn):
            total = total + got[c, k - 1]
        out[:, cols(c)] = total.astype(out.dtype)
        for k in range(1, nl):
            within(c, k).wait_send()
        for k in range(1, nn):
            along(c, k).wait_send()


def sems(*shape):
    return pltpu.SemaphoreType.DMA(shape)


def local(tokens, routes, route_weights, w_gate, w_up, w_down):
    nn, nl = lax.axis_size("node"), lax.axis_size("local")
    mn, ml = lax.axis_index("node"), lax.axis_index("local")
    devices = nn * nl
    exp_dev = w_gate.shape[0]
    experts = exp_dev * devices
    assert exp_dev == 1
    tok_dev, width = tokens.shape
    topk = routes.shape[1]
    cap = 4 * tok_dev * topk // (3 * experts)
    rows = nn * cap
    nch = chunks_of(width)
    ch = width // nch
    f32, bf16 = jnp.float32, jnp.bfloat16

    both = jnp.concatenate([routes.astype(f32), route_weights], axis=1)
    every = lax.all_gather(both, ("node", "local"), axis=0, tiled=True)
    every_routes = every[:, :topk].astype(jnp.int32)
    labels = jnp.arange(experts, dtype=jnp.int32)
    hit = every_routes[:, :, None] == labels[None, None, :]
    counts = jnp.sum(hit.astype(f32), axis=(0, 1))
    sums = jnp.sum(jnp.where(hit, every[:, topk:, None], 0.0), axis=(0, 1))
    total = jnp.float32(tok_dev * devices)
    balance_loss = jnp.sum(counts * sums) * jnp.float32(experts) / (jnp.float32(topk) * total * total)

    line = lax.dynamic_index_in_dim(every.reshape(nn, nl, tok_dev, 2 * topk), ml, 1, keepdims=False)
    plane = mn * nl + jnp.arange(nl, dtype=jnp.int32)
    chosen = line[..., :topk, None].astype(jnp.int32) == plane
    named = jnp.any(chosen, axis=2)
    weight = jnp.sum(jnp.where(chosen, line[..., topk:, None], 0.0), axis=2)
    before = jnp.tril(jnp.ones((tok_dev, tok_dev), bf16), -1)
    slot = jnp.einsum("ut,pte->pue", before, named.astype(bf16), preferred_element_type=f32)
    slot = jnp.where(named, slot.astype(jnp.int32), -1)
    where = (
        (slot.transpose(2, 0, 1)[:, None, None] == jnp.arange(cap)[None, None, :, None, None])
        & (jnp.arange(nn)[:, None] == jnp.arange(nn)[None, :])[None, :, None, :, None]
    )
    pick = where.astype(bf16).reshape(nl * rows, nn * tok_dev)
    back = (
        (slot[:, :, :, None, None] == jnp.arange(cap)[None, None, None, None, :])
        & (jnp.arange(nn)[:, None] == jnp.arange(nn)[None, :])[:, None, None, :, None]
    )
    high = lax.reduce_precision(weight, 8, 7)
    middle = lax.reduce_precision(weight - high, 8, 7)
    low = lax.reduce_precision(weight - high - middle, 8, 7)
    mix = jnp.where(back[None], jnp.stack([high, middle, low])[..., None, None], 0.0).astype(bf16)
    mix = mix.reshape(3 * nn * tok_dev, nl * rows)

    vmem = pl.BlockSpec(memory_space=pltpu.VMEM)
    hbm = pl.BlockSpec(memory_space=pl.ANY)
    got = pl.pallas_call(
        functools.partial(dispatch_kernel, nn, nl, nch),
        out_shape=jax.ShapeDtypeStruct((nl, rows, width), bf16),
        in_specs=[vmem, vmem],
        out_specs=hbm,
        scratch_shapes=[
            pltpu.VMEM((nch, nn * tok_dev, ch), bf16),
            pltpu.VMEM((nch, nl * rows, ch), bf16),
            sems(nch, nn - 1),
            sems(nch, nn - 1),
            sems(nch, nl - 1),
            sems(nch, nl - 1),
            sems(nch),
        ],
        compiler_params=pltpu.CompilerParams(
            collective_id=0, has_side_effects=True, vmem_limit_bytes=VMEM_LIMIT
        ),
    )(tokens, pick)
    got = got.reshape(nl * rows, width)
    gate = jnp.dot(got, w_gate[0], preferred_element_type=f32)
    upper = jnp.dot(got, w_up[0], preferred_element_type=f32)
    hidden = (jax.nn.silu(gate) * upper).astype(bf16)
    y = jnp.dot(hidden, w_down[0], preferred_element_type=f32).astype(bf16)

    mixed = pl.pallas_call(
        functools.partial(return_kernel, nn, nl, nch),
        out_shape=jax.ShapeDtypeStruct((tok_dev, width), bf16),
        in_specs=[hbm, vmem],
        out_specs=vmem,
        scratch_shapes=[
            pltpu.VMEM((nch, nl * rows, ch), bf16),
            pltpu.VMEM((nch, nn * tok_dev, ch), f32),
            pltpu.VMEM((nch, nn - 1, tok_dev, ch), f32),
            sems(nch, nl - 1),
            sems(nch, nl - 1),
            sems(nch, nn - 1),
            sems(nch, nn - 1),
            sems(nch),
        ],
        compiler_params=pltpu.CompilerParams(
            collective_id=1, has_side_effects=True, vmem_limit_bytes=VMEM_LIMIT
        ),
    )(y.reshape(nl, rows, width), mix)
    return (mixed, balance_loss)


def solution(mesh):
    placed = (
        P(("node", "local"), None),
        P(("node", "local"), None),
        P(("node", "local"), None),
        P(("node", "local"), None, None),
        P(("node", "local"), None, None),
        P(("node", "local"), None, None),
    )
    return jax.shard_map(
        local,
        mesh=mesh,
        in_specs=placed,
        out_specs=(P(("node", "local"), None), P()),
        check_vma=False,
    )
```

profile of v0, /device:TPU:0, one launch (start us, length us, event | category | flops | bytes accessed | tf_op | source)
XLA Modules:
  0.0 496.9 jit_solution(16565919698793316753)
XLA Ops:
  0.6 0.7 convert_element_type.44
  1.3 0.7 pad_maximum_fusion.1
  2.0 43.9 %all_gather.3 = f32[4096,12]{0,1:T(8,128)S(1)} all-gather(f32[128,12]{0,1:T(8,128)S(1)} %pad_maximum_fusion.1), channel_id=1, replica_groups=mesh['node'=4,'local'=8] {'node','local'}, dimensions={0}, use_global_device_ids=true | all-gather | bytes 202752 | tf_op jit(solution)/shard_map/all_gather | solution.py:190
  46.0 0.1 copy.30
  46.1 0.1 compare_reduce_fusion
  46.2 0.2 bitcast_select_fusion.1
  46.4 0.1 iota_compare_fusion.2
  46.6 0.7 and_convert_fusion
  47.3 1.2 copy.33
  48.4 151.5 %shard_map.77 = bf16[8,128,5120]{2,1,0:T(8,128)(2,1)} custom-call(bf16[128,5120]{1,0:T(8,128)(2,1)} %tok.1, bf16[1024,512]{1,0:T(8,128)(2,1)} %bitcast.61), custom_call_target="tpu_custom_call" | custom-call | tf_op jit(solution)/shard_map/pallas_call | solution.py:224
  200.0 12.4 %fusion.1 = f32[1024,768]{1,0:T(8,128)S(1)} fusion(bf16[1024,5120]{1,0:T(8,128)(2,1)} %bitcast.59, bf16[1,5120,768]{2,1,0:T(8,128)(2,1)} %param.10), kind=kOutput, calls=%fused_computation.2 | convolution fusion | flops 8053063680 | bytes 21495808 | tf_op jit(solution)/shard_map/dot_general | solution.py:244
  212.4 10.8 %multiply_convert_fusion = bf16[1024,768]{1,0:T(8,128)(2,1)S(1)} fusion(f32[1024,768]{1,0:T(8,128)S(1)} %fusion.1, bf16[1024,5120]{1,0:T(8,128)(2,1)S(1)} %bitcast.60, bf16[1,5120,768]{2,1,0:T(8,128)(2,1)} %param.9), kind=kOutput, calls=%fused_computation.10 | convolution fusion | flops 8057782272 | bytes 23068672 | tf_op jit(solution)/shard_map/dot_general | solution.py:243
  223.2 10.9 %convolution_convert_fusion = bf16[1024,5120]{1,0:T(8,128)(2,1)} fusion(bf16[1024,768]{1,0:T(8,128)(2,1)S(1)} %multiply_convert_fusion, bf16[1,768,5120]{2,1,0:T(8,128)(2,1)S(1)} %bitcast.67), kind=kOutput, calls=%fused_computation | convolution fusion | flops 8058306560 | bytes 19922944 | tf_op jit(solution)/shard_map/dot_general | solution.py:246
  234.1 0.1 fusion.7
  234.3 0.1 copy.25
  234.4 0.1 iota_compare_fusion.1
  234.5 0.7 broadcast_and_fusion
  235.2 2.4 select_convert_fusion
  237.7 2.7 convert_element_type.54
  240.4 4.7 copy.28.mix
  245.1 245.7 %shard_map.78 = bf16[128,5120]{1,0:T(8,128)(2,1)} custom-call(bf16[8,128,5120]{2,1,0:T(8,128)(2,1)} %bitcast.58, bf16[1536,1024]{1,0:T(8,128)(2,1)} %copy.28.mix), custom_call_target="tpu_custom_call" | custom-call | tf_op jit(solution)/shard_map/pallas_call | solution.py:248
  490.8 1.2 select_reduce_fusion
  492.0 0.6 multiply_reduce_fusion
  493.3 2.5 copy.35
  (22 shorter events, 0.2 us)
Async XLA Ops:
  200.0 12.4 %copy-start = (bf16[8,128,5120]{2,1,0:T(8,128)(2,1)S(1)}, bf16[8,128,5120]{2,1,0:T(8,128)(2,1)}, u32[]{:S(2)}) copy-start(bf16[8,128,5120]{2,1,0:T(8,128)(2,1)} %shard_map.77) | copy-start | bytes 31457284
  200.0 23.2 %slice-start = ((s8[7864320]{0:T(1024)(128)(4,1)}), s8[4194304]{0:T(1024)(128)(4,1)S(1)}, s32[]{:S(2)}) async-start(s8[7864320]{0:T(1024)(128)(4,1)} %bitcast.66), calls=%async_computation | async-start | bytes 8388608
  212.4 10.8 %slice-start.1 = ((s8[7864320]{0:T(1024)(128)(4,1)}), s8[3670016]{0:T(1024)(128)(4,1)S(1)}, s32[]{:S(2)}) async-start(s8[7864320]{0:T(1024)(128)(4,1)} %bitcast.66), calls=%async_computation.1 | async-start | bytes 7340032
where the time goes:
time: 505 us; the launch traced here: 497 us
  Pallas kernels  397 us (79%)
  blocking collectives  43.9 us (9%)
  matrix products  34.2 us (7%)
  local copies, waits for them, and re-layouts  11.3 us (2%)
  other arithmetic  7.54 us (1%)
    pallas_call x1, Pallas kernels, local(): pl.pallas_call(functools.partial(return_kernel, nn, nl, nch), out_shape=j...  246 us
    pallas_call x1, Pallas kernels, local(): pl.pallas_call(functools.partial(dispatch_kernel, nn, nl, nch), out_shape...  152 us
    all_gather x1, blocking collectives, local(): every = lax.all_gather(both, ('node', 'local'), axis=0, tiled=True)  43.9 us
    dot_general x1, matrix products, local(): upper = jnp.dot(got, w_up[0], preferred_element_type=f32)  12.4 us
    dot_general x1, matrix products, local(): y = jnp.dot(hidden, w_down[0], preferred_element_type=f32).astype(bf16)  10.9 us
    dot_general x1, matrix products, local(): gate = jnp.dot(got, w_gate[0], preferred_element_type=f32)  10.8 us

commit v1 on v0

v1 whole, which is shorter than its diff:
```python
import functools

import jax
import jax.numpy as jnp
from jax import lax
from jax.experimental import pallas as pl
from jax.experimental.pallas import tpu as pltpu
from jax.sharding import PartitionSpec as P

MESH = pl.DeviceIdType.MESH
VMEM_LIMIT = 63 * 1024 * 1024
F32, BF16, I16 = jnp.float32, jnp.bfloat16, jnp.int16
AHEAD = 2
LAG = 2


def chunks_of(width):
    return max(n for n in range(1, 11) if width % (n * 128) == 0)


def tile_of(rows):
    return max(n for n in (256, 128, 64, 32, 16, 8) if rows % n == 0)


def greet(nn, nl, mn, ml):
    barrier = pltpu.get_barrier_semaphore()
    for k in range(1, nn):
        pl.semaphore_signal(barrier, inc=1, device_id={"node": lax.rem(mn + k, nn)}, device_id_type=MESH)
    for k in range(1, nl):
        pl.semaphore_signal(barrier, inc=1, device_id={"local": lax.rem(ml + k, nl)}, device_id_type=MESH)
    pl.semaphore_wait(barrier, nn + nl - 2)


def places(info, mn, nl, topk):
    lines = info.shape[-1]
    expert = lax.broadcasted_iota(jnp.int32, (nl, lines), 0).astype(F32) + (mn * nl).astype(F32)
    named = jnp.zeros((nl, lines), F32)
    weight = jnp.zeros((nl, lines), F32)
    for k in range(topk):
        match = info[k : k + 1, :] == expert
        named = jnp.where(match, 1.0, named)
        weight = jnp.where(match, info[8 + k : 9 + k, :], weight)
    earlier = (
        lax.broadcasted_iota(jnp.int32, (lines, lines), 0) < lax.broadcasted_iota(jnp.int32, (lines, lines), 1)
    ).astype(F32)
    slot = jnp.dot(named, earlier, preferred_element_type=F32)
    return jnp.where(named > 0.0, slot, -1.0), weight


def dispatch_kernel(
    nn, nl, nch, cap, topk,
    tok, routes, gains, wg, wu,
    hid, infos_out, loss,
    held, sent, arrived, acc, wbuf, pick, turned, infos, tallies, tally,
    up_send, up_recv, dn_send, dn_recv, p_send, p_recv, i_send, i_recv, t_send, t_recv, own_sem, w_sem,
):
    mn, ml = lax.axis_index("node"), lax.axis_index("local")
    lines, width = tok.shape
    ch = width // nch
    ff = wg.shape[1]
    rows = nn * cap
    experts = nn * nl

    def cols(c):
        return pl.ds(pl.multiple_of(c * ch, 128), ch)

    def own(c):
        return pltpu.make_async_copy(tok.at[:, cols(c)], held.at[c, mn], own_sem.at[c])

    def weights(c):
        at = pl.ds(pl.multiple_of(c * ch, 128), ch)
        return (
            pltpu.make_async_copy(wg.at[at, :], wbuf.at[c, :, pl.ds(0, ff)], w_sem.at[c, 0]),
            pltpu.make_async_copy(wu.at[at, :], wbuf.at[c, :, pl.ds(ff, ff)], w_sem.at[c, 1]),
        )

    def up(c, d, block):
        return pltpu.make_async_remote_copy(
            src_ref=held.at[c, block], dst_ref=held.at[c, block],
            send_sem=up_send.at[c, d], recv_sem=up_recv.at[c, d],
            device_id={"node": mn + 1}, device_id_type=MESH,
        )

    def down(c, d, block):
        return pltpu.make_async_remote_copy(
            src_ref=held.at[c, block], dst_ref=held.at[c, block],
            send_sem=dn_send.at[c, d], recv_sem=dn_recv.at[c, d],
            device_id={"node": mn - 1}, device_id_type=MESH,
        )

    def slots_of(e):
        return pl.ds(pl.multiple_of(e * cap, cap), cap)

    def within(c, n, k):
        e = lax.rem(ml + k, nl)
        return pltpu.make_async_remote_copy(
            src_ref=sent.at[c, n, slots_of(e), :],
            dst_ref=arrived.at[c, pl.ds(pl.multiple_of(ml * rows + n * cap, cap), cap), :],
            send_sem=p_send.at[c, k - 1], recv_sem=p_recv.at[c, k - 1],
            device_id={"local": e}, device_id_type=MESH,
        )

    def within_all(c, k):
        l = lax.rem(ml + nl - k, nl)
        at = arrived.at[c, pl.ds(pl.multiple_of(l * rows, rows), rows), :]
        return pltpu.make_async_remote_copy(
            src_ref=at, dst_ref=at, send_sem=p_send.at[c, k - 1], recv_sem=p_recv.at[c, k - 1],
            device_id={"local": l}, device_id_type=MESH,
        )

    def info_copy(k):
        return pltpu.make_async_remote_copy(
            src_ref=infos.at[mn], dst_ref=infos.at[mn], send_sem=i_send.at[k - 1], recv_sem=i_recv.at[k - 1],
            device_id={"node": lax.rem(mn + k, nn)}, device_id_type=MESH,
        )

    def tally_copy(k):
        return pltpu.make_async_remote_copy(
            src_ref=tally, dst_ref=tallies.at[ml], send_sem=t_send.at[k - 1], recv_sem=t_recv.at[k - 1],
            device_id={"local": lax.rem(ml + k, nl)}, device_id_type=MESH,
        )

    def start_own(c):
        @pl.when(mn + 1 < nn)
        def _():
            up(c, 0, mn).start()

        @pl.when(mn > 0)
        def _():
            down(c, 0, mn).start()

    @pl.loop(0, nch)
    def _(c):
        own(c).start()

    @pl.loop(0, nch)
    def _(c):
        for copy in weights(c):
            copy.start()

    turned[...] = jnp.zeros(turned.shape, F32)
    named = routes[...].astype(F32)
    turned[:, 0:topk] = named
    turned[:, 8 : 8 + topk] = gains[...]
    infos[mn, 0:16, :] = turned[...].T[0:16, :]
    label = lax.broadcasted_iota(jnp.int32, (lines, tally.shape[1]), 1)
    hits = jnp.zeros(label.shape, F32)
    sums = jnp.zeros(label.shape, F32)
    for k in range(topk):
        match = routes[:, k : k + 1] == label
        hits = hits + jnp.where(match, 1.0, 0.0)
        sums = sums + jnp.where(match, gains[:, k : k + 1], 0.0)
    line = lax.broadcasted_iota(jnp.int32, (8, tally.shape[1]), 0)
    infos[mn, 16:24, :] = jnp.where(
        line == 0, jnp.sum(hits, axis=0, keepdims=True), jnp.where(line == 1, jnp.sum(sums, axis=0, keepdims=True), 0.0)
    )

    greet(nn, nl, mn, ml)
    for k in range(1, nn):
        info_copy(k).start()

    @pl.loop(0, nch)
    def _(c):
        own(c).wait()

        @pl.when(c < AHEAD)
        def _():
            start_own(c)

    def picks(n):
        slot, _ = places(infos[n], mn, nl, topk)
        rank = lax.broadcasted_iota(jnp.int32, (cap, lines), 0).astype(F32)
        for e in range(nl):
            pick[n, e * cap : (e + 1) * cap, :] = jnp.where(slot[e : e + 1, :] == rank, 1.0, 0.0).astype(BF16)

    def hand_out(c, n):
        picked = jnp.dot(pick[n], held[c, n], preferred_element_type=F32)
        sent[c, n] = picked.astype(BF16)
        for k in range(1, nl):
            within(c, n, k).start()
        arrived[c, pl.ds(pl.multiple_of(ml * rows + n * cap, cap), cap), :] = sent[c, n, slots_of(ml), :]

    picks(mn)

    @pl.loop(0, nch)
    def _(c):
        hand_out(c, mn)

    for k in range(1, nn):
        info_copy(k).wait_recv()
    total = infos[0, 16:24, :]
    for n in range(1, nn):
        total = total + infos[n, 16:24, :]
    tally[...] = total
    tallies[ml] = total
    for k in range(1, nl):
        tally_copy(k).start()

    @pl.loop(0, nn)
    def _(n):
        @pl.when(n != mn)
        def _():
            picks(n)

    acc[...] = jnp.zeros(acc.shape, F32)
    step = tile_of(nl * rows)

    def multiply(c):
        for copy in weights(c):
            copy.wait()
        for k in range(1, nl):
            within_all(c, k).wait_recv()

        @pl.loop(0, nl * rows // step)
        def _(m):
            at = pl.ds(pl.multiple_of(m * step, step), step)
            acc[at, :] += jnp.dot(arrived[c, at, :], wbuf[c], preferred_element_type=F32)

    @pl.loop(0, nch + LAG)
    def _(i):
        @pl.when(i < nch)
        def _():
            @pl.when(i + AHEAD < nch)
            def _():
                start_own(i + AHEAD)

            for d in range(nn - 1):
                @pl.when(mn - 1 - d >= 0)
                def _():
                    block = mn - 1 - d
                    up(i, d, block).wait_recv()

                    if d + 1 < nn - 1:
                        @pl.when(mn + 1 < nn)
                        def _():
                            up(i, d + 1, block).start()

                @pl.when(mn + 1 + d < nn)
                def _():
                    block = mn + 1 + d
                    down(i, d, block).wait_recv()

                    if d + 1 < nn - 1:
                        @pl.when(mn > 0)
                        def _():
                            down(i, d + 1, block).start()

            @pl.loop(0, nn)
            def _(n):
                @pl.when(n != mn)
                def _():
                    hand_out(i, n)

        @pl.when(i >= LAG)
        def _():
            multiply(i - LAG)

    @pl.loop(0, nl * rows // step)
    def _(m):
        at = pl.ds(pl.multiple_of(m * step, step), step)
        gate = acc[at, 0:ff]
        hid[at, :] = (gate / (1.0 + jnp.exp(-gate)) * acc[at, ff : 2 * ff]).astype(BF16)

    infos_out[...] = infos[...]
    for k in range(1, nl):
        tally_copy(k).wait_recv()
    total = tallies[0]
    for l in range(1, nl):
        total = total + tallies[l]
    tokens = float(lines * experts)
    loss[...] = jnp.sum(total[0:1, :] * total[1:2, :], axis=1, keepdims=True) * (experts / (topk * tokens * tokens))

    for k in range(1, nn):
        info_copy(k).wait_send()
    for k in range(1, nl):
        tally_copy(k).wait_send()

    @pl.loop(0, nch)
    def _(c):
        for k in range(1, nl):
            within_all(c, k).wait_send()
        for d in range(nn - 1):
            @pl.when((mn + 1 < nn) & (mn - d >= 0))
            def _():
                up(c, d, mn - d).wait_send()

            @pl.when((mn > 0) & (mn + d < nn))
            def _():
                down(c, d, mn + d).wait_send()


def return_kernel(
    nn, nl, nch, cap, topk,
    hid, infos, wd,
    out,
    wbuf, y, held, mix, part, scale, base, got, got_scale,
    p_send, p_recv, z_send, z_recv, s_send, s_recv, w_sem,
):
    mn, ml = lax.axis_index("node"), lax.axis_index("local")
    lines, width = out.shape
    ch = width // nch
    rows = nn * cap
    step = tile_of(nl * rows)

    def cols(c):
        return pl.ds(pl.multiple_of(c * ch, 128), ch)

    def weights(c):
        return pltpu.make_async_copy(wd.at[:, cols(c)], wbuf.at[c], w_sem.at[c])

    def slots_of(e):
        return pl.ds(pl.multiple_of(e * cap, cap), cap)

    def within(c, n, k):
        l = lax.rem(ml + k, nl)
        return pltpu.make_async_remote_copy(
            src_ref=y.at[c, pl.ds(pl.multiple_of(l * rows + n * cap, cap), cap), :],
            dst_ref=held.at[c, n, slots_of(ml), :],
            send_sem=p_send.at[c, k - 1], recv_sem=p_recv.at[c, k - 1],
            device_id={"local": l}, device_id_type=MESH,
        )

    def within_all(c, k):
        l = lax.rem(ml + k, nl)
        at = y.at[c, pl.ds(pl.multiple_of(l * rows, rows), rows), :]
        return pltpu.make_async_remote_copy(
            src_ref=at, dst_ref=at, send_sem=p_send.at[c, k - 1], recv_sem=p_recv.at[c, k - 1],
            device_id={"local": l}, device_id_type=MESH,
        )

    def along(c, k):
        p = lax.rem(mn + k, nn)
        return (
            pltpu.make_async_remote_copy(
                src_ref=part.at[c, k - 1], dst_ref=got.at[c, k - 1],
                send_sem=z_send.at[c, k - 1], recv_sem=z_recv.at[c, k - 1],
                device_id={"node": p}, device_id_type=MESH,
            ),
            pltpu.make_async_remote_copy(
                src_ref=scale.at[c, k - 1], dst_ref=got_scale.at[c, k - 1],
                send_sem=s_send.at[c, k - 1], recv_sem=s_recv.at[c, k - 1],
                device_id={"node": p}, device_id_type=MESH,
            ),
        )

    @pl.loop(0, nch)
    def _(c):
        weights(c).start()

    greet(nn, nl, mn, ml)

    @pl.loop(0, nch)
    def _(c):
        weights(c).wait()

        @pl.loop(0, nl * rows // step)
        def _(m):
            at = pl.ds(pl.multiple_of(m * step, step), step)
            y[c, at, :] = jnp.dot(hid[at, :], wbuf[c], preferred_element_type=F32).astype(BF16)

        for k in range(1, nl):
            for n in range(nn):
                within(c, n, k).start()
        for n in range(nn):
            held[c, n, slots_of(ml), :] = y[c, pl.ds(pl.multiple_of(ml * rows + n * cap, cap), cap), :]

    @pl.loop(0, nn)
    def _(n):
        slot, weight = places(infos[n], mn, nl, topk)
        rank = lax.broadcasted_iota(jnp.int32, (cap, lines), 0).astype(F32)
        back = jnp.concatenate(
            [jnp.where(slot[e : e + 1, :] == rank, weight[e : e + 1, :], 0.0) for e in range(nl)], axis=0
        ).T
        high = back.astype(BF16)
        rest = back - high.astype(F32)
        middle = rest.astype(BF16)
        low = (rest - middle.astype(F32)).astype(BF16)
        mix[n, 0:lines, :] = high
        mix[n, lines : 2 * lines, :] = middle
        mix[n, 2 * lines : 3 * lines, :] = low

    diagonal = lax.broadcasted_iota(jnp.int32, (lines, lines), 0) == lax.broadcasted_iota(jnp.int32, (lines, lines), 1)

    def blend(c, n):
        terms = jnp.dot(mix[n], held[c, n], preferred_element_type=F32)
        return terms[0:lines] + terms[lines : 2 * lines] + terms[2 * lines : 3 * lines]

    @pl.loop(0, nch)
    def _(c):
        for k in range(1, nl):
            within_all(c, k).wait_recv()
        for k in range(1, nn):
            value = blend(c, lax.rem(mn + k, nn))
            peak = jnp.maximum(jnp.max(jnp.abs(value), axis=1, keepdims=True), 1e-30)
            part[c, k - 1] = jnp.round(value * (32767.0 / peak)).astype(jnp.int32).astype(I16)
            scale[c, k - 1] = jnp.broadcast_to(
                jnp.sum(jnp.where(diagonal, peak, 0.0), axis=0, keepdims=True), (8, lines)
            )
            for copy in along(c, k):
                copy.start()
        base[c] = blend(c, mn)

    @pl.loop(0, nch)
    def _(c):
        total = base[c]
        for k in range(1, nn):
            for copy in along(c, k):
                copy.wait_recv()
            peak = jnp.sum(jnp.where(diagonal, got_scale[c, k - 1, 0:1, :], 0.0), axis=1, keepdims=True)
            total = total + got[c, k - 1].astype(jnp.int32).astype(F32) * (peak * (1.0 / 32767.0))
        out[:, cols(c)] = total.astype(out.dtype)
        for k in range(1, nl):
            within_all(c, k).wait_send()
        for k in range(1, nn):
            for copy in along(c, k):
                copy.wait_send()


def sems(*shape):
    return pltpu.SemaphoreType.DMA(shape)


def local(tokens, routes, route_weights, w_gate, w_up, w_down):
    nn, nl = lax.axis_size("node"), lax.axis_size("local")
    exp_dev, width, ff = w_gate.shape
    experts = exp_dev * nn * nl
    assert exp_dev == 1
    lines, topk = routes.shape
    assert topk <= 8
    cap = 4 * lines * topk // (3 * experts)
    rows = nn * cap
    nch = chunks_of(width)
    ch = width // nch
    wide = -(-experts // 128) * 128
    assert wide == lines

    vmem = pl.BlockSpec(memory_space=pltpu.VMEM)
    hbm = pl.BlockSpec(memory_space=pl.ANY)
    hidden, infos, loss = pl.pallas_call(
        functools.partial(dispatch_kernel, nn, nl, nch, cap, topk),
        out_shape=(
            jax.ShapeDtypeStruct((nl * rows, ff), BF16),
            jax.ShapeDtypeStruct((nn, 24, lines), F32),
            jax.ShapeDtypeStruct((1, 1), F32),
        ),
        in_specs=[hbm, vmem, vmem, hbm, hbm],
        out_specs=(vmem, vmem, vmem),
        scratch_shapes=[
            pltpu.VMEM((nch, nn, lines, ch), BF16),
            pltpu.VMEM((nch, nn, nl * cap, ch), BF16),
            pltpu.VMEM((nch, nl * rows, ch), BF16),
            pltpu.VMEM((nl * rows, 2 * ff), F32),
            pltpu.VMEM((nch, ch, 2 * ff), BF16),
            pltpu.VMEM((nn, nl * cap, lines), BF16),
            pltpu.VMEM((lines, 128), F32),
            pltpu.VMEM((nn, 24, lines), F32),
            pltpu.VMEM((nl, 8, wide), F32),
            pltpu.VMEM((8, wide), F32),
            sems(nch, nn - 1), sems(nch, nn - 1), sems(nch, nn - 1), sems(nch, nn - 1),
            sems(nch, nl - 1), sems(nch, nl - 1),
            sems(nn - 1), sems(nn - 1), sems(nl - 1), sems(nl - 1),
            sems(nch), sems(nch, 2),
        ],
        compiler_params=pltpu.CompilerParams(collective_id=0, has_side_effects=True, vmem_limit_bytes=VMEM_LIMIT),
    )(tokens, routes, route_weights, w_gate[0], w_up[0])

    mixed = pl.pallas_call(
        functools.partial(return_kernel, nn, nl, nch, cap, topk),
        out_shape=jax.ShapeDtypeStruct((lines, width), tokens.dtype),
        in_specs=[vmem, vmem, hbm],
        out_specs=vmem,
        scratch_shapes=[
            pltpu.VMEM((nch, ff, ch), BF16),
            pltpu.VMEM((nch, nl * rows, ch), BF16),
            pltpu.VMEM((nch, nn, nl * cap, ch), BF16),
            pltpu.VMEM((nn, 3 * lines, nl * cap), BF16),
            pltpu.VMEM((nch, nn - 1, lines, ch), I16),
            pltpu.VMEM((nch, nn - 1, 8, lines), F32),
            pltpu.VMEM((nch, lines, ch), F32),
            pltpu.VMEM((nch, nn - 1, lines, ch), I16),
            pltpu.VMEM((nch, nn - 1, 8, lines), F32),
            sems(nch, nl - 1), sems(nch, nl - 1),
            sems(nch, nn - 1), sems(nch, nn - 1), sems(nch, nn - 1), sems(nch, nn - 1),
            sems(nch),
        ],
        compiler_params=pltpu.CompilerParams(collective_id=1, has_side_effects=True, vmem_limit_bytes=VMEM_LIMIT),
    )(hidden, infos, w_down[0])
    return (mixed, loss.reshape(()))


def solution(mesh):
    placed = (
        P(("node", "local"), None),
        P(("node", "local"), None),
        P(("node", "local"), None),
        P(("node", "local"), None, None),
        P(("node", "local"), None, None),
        P(("node", "local"), None, None),
    )
    return jax.shard_map(
        local,
        mesh=mesh,
        in_specs=placed,
        out_specs=(P(("node", "local"), None), P()),
        check_vma=False,
    )
```

time: 505 us -> 281 us (0.56); the launches traced: 497 us -> 280 us
  Pallas kernels: 397 us -> 273 us
  blocking collectives: 43.9 us -> 0 us
  matrix products: 34.2 us -> 0 us
  other arithmetic: 7.54 us -> 0 us
  local copies, waits for them, and re-layouts: 11.3 us -> 5.29 us
    pallas_call x2, Pallas kernels: 397 us -> 273 us  [the longest x1 140 us: local(): pl.pallas_call(functools.partial(return_kernel, nn, nl, nch, cap, topk),...]
    all_gather x1 -> x0, blocking collectives: 43.9 us -> none  [local(): every = lax.all_gather(both, ('node', 'local'), axis=0, tiled=True)]
    dot_general x4 -> x0, matrix products: 34.2 us -> none  [the longest x1 12.4 us: local(): upper = jnp.dot(got, w_up[0], preferred_element_type=f32)]
    convert_element_type x3 -> x0, local copies, waits for them, and re-layouts: 7.44 us -> none  [the longest x2 7.44 us: local(): jnp.where(back[None], jnp.stack([high, middle, low])[..., None, None], 0.0)]
where the time goes in v1:
time: 281 us; the launch traced here: 280 us
  Pallas kernels  273 us (97%)
  local copies, waits for them, and re-layouts  5.29 us (2%)
    pallas_call x1, Pallas kernels, local(): pl.pallas_call(functools.partial(return_kernel, nn, nl, nch, cap, topk),...  140 us
    pallas_call x1, Pallas kernels, local(): pl.pallas_call(functools.partial(dispatch_kernel, nn, nl, nch, cap, topk)...  132 us

profile of v1, /device:TPU:0, one launch (start us, length us, event | category | flops | bytes accessed | tf_op | source)
XLA Modules:
  0.0 280.3 jit_solution(7266327839165987354)
XLA Ops:
  0.6 1.4 copy.8.routes
  2.1 1.4 copy.9.gains
  3.5 132.3 %shard_map.77 = (bf16[1024,768]{1,0:T(8,128)(2,1)}, f32[4,24,128]{2,1,0:T(8,128)}, f32[1,1]{1,0:T(1,128)}) custom-call(bf16[128,5120]{1,0:T(8,128)(2,1)} %tok.1, s32[128,6]{1,0:T(8,128)} %copy.8.routes, f32[128,6]{1,0:T(8,128)} %copy.9.gains, bf16[5120,768]{1,0:T(8,128)(2,1)} %bitcast.4, bf16[5120,768]{1,0:T(8,128)(2,1)} %bitcast.5), custom_call_target="tpu_custom_call" | custom-call | tf_op jit(solution)/shard_map/pallas_call | solution.py:439
  135.8 140.3 %shard_map.78 = bf16[128,5120]{1,0:T(8,128)(2,1)} custom-call(bf16[1024,768]{1,0:T(8,128)(2,1)} %get-tuple-element.5.hid, f32[4,24,128]{2,1,0:T(8,128)} %get-tuple-element.6.infos, bf16[768,5120]{1,0:T(8,128)(2,1)} %bitcast.6), custom_call_target="tpu_custom_call" | custom-call | tf_op jit(solution)/shard_map/pallas_call | solution.py:467
  276.1 2.5 copy.12

commit v2 on v1

--- a/solution.py
+++ b/solution.py
@@ -51,7 +51,7 @@
     nn, nl, nch, cap, topk,
     tok, routes, gains, wg, wu,
     hid, infos_out, loss,
-    held, sent, arrived, acc, wbuf, pick, turned, infos, tallies, tally,
+    held, sent, arrived, acc, wbuf, pick, infos, tallies, tally,
     up_send, up_recv, dn_send, dn_recv, p_send, p_recv, i_send, i_recv, t_send, t_recv, own_sem, w_sem,
 ):
     mn, ml = lax.axis_index("node"), lax.axis_index("local")
@@ -138,21 +138,21 @@
         for copy in weights(c):
             copy.start()
 
-    turned[...] = jnp.zeros(turned.shape, F32)
-    named = routes[...].astype(F32)
-    turned[:, 0:topk] = named
-    turned[:, 8 : 8 + topk] = gains[...]
-    infos[mn, 0:16, :] = turned[...].T[0:16, :]
-    label = lax.broadcasted_iota(jnp.int32, (lines, tally.shape[1]), 1)
+    infos[mn, 0:16, :] = jnp.zeros((16, lines), F32)
+    infos[mn, 0:topk, :] = routes[...].astype(F32)
+    infos[mn, 8 : 8 + topk, :] = gains[...]
+    label = lax.broadcasted_iota(jnp.int32, (tally.shape[1], lines), 0)
     hits = jnp.zeros(label.shape, F32)
     sums = jnp.zeros(label.shape, F32)
     for k in range(topk):
-        match = routes[:, k : k + 1] == label
-        hits = hits + jnp.where(match, 1.0, 0.0)
-        sums = sums + jnp.where(match, gains[:, k : k + 1], 0.0)
+        match = routes[k : k + 1, :] == label
+        hits = jnp.where(match, 1.0, hits)
+        sums = jnp.where(match, gains[k : k + 1, :], sums)
     line = lax.broadcasted_iota(jnp.int32, (8, tally.shape[1]), 0)
     infos[mn, 16:24, :] = jnp.where(
-        line == 0, jnp.sum(hits, axis=0, keepdims=True), jnp.where(line == 1, jnp.sum(sums, axis=0, keepdims=True), 0.0)
+        line == 0,
+        jnp.sum(hits.T, axis=0, keepdims=True),
+        jnp.where(line == 1, jnp.sum(sums.T, axis=0, keepdims=True), 0.0),
     )
 
     greet(nn, nl, mn, ml)
@@ -293,8 +293,8 @@
     nn, nl, nch, cap, topk,
     hid, infos, wd,
     out,
-    wbuf, y, held, mix, part, scale, base, got, got_scale,
-    p_send, p_recv, z_send, z_recv, s_send, s_recv, w_sem,
+    wbuf, y, held, mix, work, part, scale, got, got_scale,
+    p_send, p_recv, o_send, o_recv, z_send, z_recv, s_send, s_recv, w_sem,
 ):
     mn, ml = lax.axis_index("node"), lax.axis_index("local")
     lines, width = out.shape
@@ -311,37 +311,45 @@
     def slots_of(e):
         return pl.ds(pl.multiple_of(e * cap, cap), cap)
 
-    def within(c, n, k):
+    def within(c, n, k, send, recv):
         l = lax.rem(ml + k, nl)
         return pltpu.make_async_remote_copy(
             src_ref=y.at[c, pl.ds(pl.multiple_of(l * rows + n * cap, cap), cap), :],
             dst_ref=held.at[c, n, slots_of(ml), :],
-            send_sem=p_send.at[c, k - 1], recv_sem=p_recv.at[c, k - 1],
+            send_sem=send.at[c, k - 1], recv_sem=recv.at[c, k - 1],
             device_id={"local": l}, device_id_type=MESH,
         )
 
-    def within_all(c, k):
-        l = lax.rem(ml + k, nl)
-        at = y.at[c, pl.ds(pl.multiple_of(l * rows, rows), rows), :]
+    def within_far(c, k):
+        at = y.at[c, pl.ds(0, rows - cap), :]
         return pltpu.make_async_remote_copy(
             src_ref=at, dst_ref=at, send_sem=p_send.at[c, k - 1], recv_sem=p_recv.at[c, k - 1],
-            device_id={"local": l}, device_id_type=MESH,
-        )
-
-    def along(c, k):
-        p = lax.rem(mn + k, nn)
+            device_id={"local": lax.rem(ml + k, nl)}, device_id_type=MESH,
+        )
+
+    def along(c, p, toward):
+        mine = jnp.where(p < mn, p, p - 1)
+        there = jnp.where(p > mn, p, jnp.where(p == mn - 1, nn, p))
         return (
             pltpu.make_async_remote_copy(
-                src_ref=part.at[c, k - 1], dst_ref=got.at[c, k - 1],
-                send_sem=z_send.at[c, k - 1], recv_sem=z_recv.at[c, k - 1],
-                device_id={"node": p}, device_id_type=MESH,
+                src_ref=part.at[c, mine], dst_ref=got.at[c, there],
+                send_sem=z_send.at[c, mine], recv_sem=z_recv.at[c, there],
+                device_id={"node": mn + toward}, device_id_type=MESH,
             ),
             pltpu.make_async_remote_copy(
-                src_ref=scale.at[c, k - 1], dst_ref=got_scale.at[c, k - 1],
-                send_sem=s_send.at[c, k - 1], recv_sem=s_recv.at[c, k - 1],
-                device_id={"node": p}, device_id_type=MESH,
+                src_ref=scale.at[c, mine], dst_ref=got_scale.at[c, there],
+                send_sem=s_send.at[c, mine], recv_sem=s_recv.at[c, there],
+                device_id={"node": mn + toward}, device_id_type=MESH,
             ),
         )
+
+    def land(c, slot, toward):
+        for buffer, sem in ((got, z_recv), (got_scale, s_recv)):
+            pltpu.make_async_remote_copy(
+                src_ref=buffer.at[c, slot], dst_ref=buffer.at[c, slot],
+                send_sem=sem.at[c, slot], recv_sem=sem.at[c, slot],
+                device_id={"node": mn - toward}, device_id_type=MESH,
+            ).wait_recv()
 
     @pl.loop(0, nch)
     def _(c):
@@ -359,10 +367,15 @@
             y[c, at, :] = jnp.dot(hid[at, :], wbuf[c], preferred_element_type=F32).astype(BF16)
 
         for k in range(1, nl):
-            for n in range(nn):
-                within(c, n, k).start()
+            for j in range(1, nn):
+                within(c, lax.rem(mn + j, nn), k, p_send, p_recv).start()
         for n in range(nn):
             held[c, n, slots_of(ml), :] = y[c, pl.ds(pl.multiple_of(ml * rows + n * cap, cap), cap), :]
+
+    @pl.loop(0, nch)
+    def _(c):
+        for k in range(1, nl):
+            within(c, mn, k, o_send, o_recv).start()
 
     @pl.loop(0, nn)
     def _(n):
@@ -385,35 +398,77 @@
         terms = jnp.dot(mix[n], held[c, n], preferred_element_type=F32)
         return terms[0:lines] + terms[lines : 2 * lines] + terms[2 * lines : 3 * lines]
 
-    @pl.loop(0, nch)
-    def _(c):
-        for k in range(1, nl):
-            within_all(c, k).wait_recv()
-        for k in range(1, nn):
-            value = blend(c, lax.rem(mn + k, nn))
-            peak = jnp.maximum(jnp.max(jnp.abs(value), axis=1, keepdims=True), 1e-30)
-            part[c, k - 1] = jnp.round(value * (32767.0 / peak)).astype(jnp.int32).astype(I16)
-            scale[c, k - 1] = jnp.broadcast_to(
-                jnp.sum(jnp.where(diagonal, peak, 0.0), axis=0, keepdims=True), (8, lines)
-            )
-            for copy in along(c, k):
-                copy.start()
-        base[c] = blend(c, mn)
-
-    @pl.loop(0, nch)
-    def _(c):
-        total = base[c]
-        for k in range(1, nn):
-            for copy in along(c, k):
-                copy.wait_recv()
-            peak = jnp.sum(jnp.where(diagonal, got_scale[c, k - 1, 0:1, :], 0.0), axis=1, keepdims=True)
-            total = total + got[c, k - 1].astype(jnp.int32).astype(F32) * (peak * (1.0 / 32767.0))
-        out[:, cols(c)] = total.astype(out.dtype)
-        for k in range(1, nl):
-            within_all(c, k).wait_send()
-        for k in range(1, nn):
-            for copy in along(c, k):
-                copy.wait_send()
+    def widened(c, slot):
+        peak = jnp.sum(jnp.where(diagonal, got_scale[c, slot, 0:1, :], 0.0), axis=1, keepdims=True)
+        return got[c, slot].astype(jnp.int32).astype(F32) * (peak * (1.0 / 32767.0))
+
+    def pass_on(c, p, toward, relay):
+        work[...] = blend(c, p)
+
+        @pl.when(relay)
+        def _():
+            land(c, p, toward)
+            work[...] += widened(c, p)
+
+        value = work[...]
+        peak = jnp.maximum(jnp.max(jnp.abs(value), axis=1, keepdims=True), 1e-30)
+        mine = jnp.where(p < mn, p, p - 1)
+        part[c, mine] = jnp.round(value * (32767.0 / peak)).astype(jnp.int32).astype(I16)
+        scale[c, mine] = jnp.broadcast_to(jnp.sum(jnp.where(diagonal, peak, 0.0), axis=0, keepdims=True), (8, lines))
+        for copy in along(c, p, toward):
+            copy.start()
+
+    @pl.loop(0, nch + nn - 2)
+    def _(i):
+        @pl.when(i < nch)
+        def _():
+            for k in range(1, nl):
+                within_far(i, k).wait_recv()
+
+        c_up = i - mn
+        c_down = i - (nn - 1 - mn)
+        for d in reversed(range(nn - 1)):
+            @pl.when((c_up >= 0) & (c_up < nch) & (mn + 1 + d < nn))
+            def _():
+                pass_on(c_up, mn + 1 + d, 1, mn > 0)
+
+            @pl.when((c_down >= 0) & (c_down < nch) & (mn - 1 - d >= 0))
+            def _():
+                pass_on(c_down, mn - 1 - d, -1, mn < nn - 1)
+
+    @pl.loop(0, nch)
+    def _(c):
+        for k in range(1, nl):
+            within(c, mn, k, o_send, o_recv).wait_recv()
+        work[...] = blend(c, mn)
+
+        @pl.when(mn > 0)
+        def _():
+            land(c, mn, 1)
+            work[...] += widened(c, mn)
+
+        @pl.when(mn < nn - 1)
+        def _():
+            land(c, nn, -1)
+            work[...] += widened(c, nn)
+
+        out[:, cols(c)] = work[...].astype(out.dtype)
+
+    @pl.loop(0, nch)
+    def _(c):
+        for k in range(1, nl):
+            within_far(c, k).wait_send()
+            within(c, mn, k, o_send, o_recv).wait_send()
+        for d in range(nn - 1):
+            @pl.when(mn + 1 + d < nn)
+            def _():
+                for copy in along(c, mn + 1 + d, 1):
+                    copy.wait_send()
+
+            @pl.when(mn - 1 - d >= 0)
+            def _():
+                for copy in along(c, mn - 1 - d, -1):
+                    copy.wait_send()
 
 
 def sems(*shape):
@@ -452,7 +507,6 @@
             pltpu.VMEM((nl * rows, 2 * ff), F32),
             pltpu.VMEM((nch, ch, 2 * ff), BF16),
             pltpu.VMEM((nn, nl * cap, lines), BF16),
-            pltpu.VMEM((lines, 128), F32),
             pltpu.VMEM((nn, 24, lines), F32),
             pltpu.VMEM((nl, 8, wide), F32),
             pltpu.VMEM((8, wide), F32),
@@ -462,7 +516,7 @@
             sems(nch), sems(nch, 2),
         ],
         compiler_params=pltpu.CompilerParams(collective_id=0, has_side_effects=True, vmem_limit_bytes=VMEM_LIMIT),
-    )(tokens, routes, route_weights, w_gate[0], w_up[0])
+    )(tokens, routes.T, route_weights.T, w_gate[0], w_up[0])
 
     mixed = pl.pallas_call(
         functools.partial(return_kernel, nn, nl, nch, cap, topk),
@@ -474,13 +528,13 @@
             pltpu.VMEM((nch, nl * rows, ch), BF16),
             pltpu.VMEM((nch, nn, nl * cap, ch), BF16),
             pltpu.VMEM((nn, 3 * lines, nl * cap), BF16),
+            pltpu.VMEM((lines, ch), F32),
             pltpu.VMEM((nch, nn - 1, lines, ch), I16),
             pltpu.VMEM((nch, nn - 1, 8, lines), F32),
-            pltpu.VMEM((nch, lines, ch), F32),
-            pltpu.VMEM((nch, nn - 1, lines, ch), I16),
-            pltpu.VMEM((nch, nn - 1, 8, lines), F32),
-            sems(nch, nl - 1), sems(nch, nl - 1),
-            sems(nch, nn - 1), sems(nch, nn - 1), sems(nch, nn - 1), sems(nch, nn - 1),
+            pltpu.VMEM((nch, nn + 1, lines, ch), I16),
+            pltpu.VMEM((nch, nn + 1, 8, lines), F32),
+            sems(nch, nl - 1), sems(nch, nl - 1), sems(nch, nl - 1), sems(nch, nl - 1),
+            sems(nch, nn - 1), sems(nch, nn + 1), sems(nch, nn - 1), sems(nch, nn + 1),
             sems(nch),
         ],
         compiler_params=pltpu.CompilerParams(collective_id=1, has_side_effects=True, vmem_limit_bytes=VMEM_LIMIT),

time: 281 us -> 263 us (0.936)
  Pallas kernels: 273 us -> 258 us
  local copies, waits for them, and re-layouts: 5.29 us -> 2.46 us
    pallas_call x1, Pallas kernels: 140 us -> 127 us  [local(): pl.pallas_call(functools.partial(return_kernel, nn, nl, nch, cap, topk),...]
    unnamed x3 -> x1, local copies, waits for them, and re-layouts: 5.29 us -> 2.46 us
where the time goes in v2:
time: 263 us
  Pallas kernels  258 us (98%)
    pallas_call x1, Pallas kernels, local(): pl.pallas_call(functools.partial(dispatch_kernel, nn, nl, nch, cap, topk)...  132 us
    pallas_call x1, Pallas kernels, local(): pl.pallas_call(functools.partial(return_kernel, nn, nl, nch, cap, topk),...  127 us

profile of v2, /device:TPU:0, one launch (start us, length us, event | category | flops | bytes accessed | tf_op | source)
XLA Modules:
  0.0 263.0 jit_solution(6897595952812396276)
XLA Ops:
  0.6 131.6 %shard_map.77 = (bf16[1024,768]{1,0:T(8,128)(2,1)}, f32[4,24,128]{2,1,0:T(8,128)}, f32[1,1]{1,0:T(1,128)}) custom-call(bf16[128,5120]{1,0:T(8,128)(2,1)} %tok.1, s32[6,128]{1,0:T(8,128)} %bitcast.9, f32[6,128]{1,0:T(8,128)} %bitcast.10, bf16[5120,768]{1,0:T(8,128)(2,1)} %bitcast.6, bf16[5120,768]{1,0:T(8,128)(2,1)} %bitcast.7), custom_call_target="tpu_custom_call" | custom-call | tf_op jit(solution)/shard_map/pallas_call | solution.py:494
  132.3 126.5 %shard_map.78 = bf16[128,5120]{1,0:T(8,128)(2,1)} custom-call(bf16[1024,768]{1,0:T(8,128)(2,1)} %get-tuple-element.5.hid, f32[4,24,128]{2,1,0:T(8,128)} %get-tuple-element.6.infos, bf16[768,5120]{1,0:T(8,128)(2,1)} %bitcast.8), custom_call_target="tpu_custom_call" | custom-call | tf_op jit(solution)/shard_map/pallas_call | solution.py:521
  258.8 2.5 copy.10

commit v3 on v0

v3 whole, which is shorter than its diff:
```python
import functools

import jax
import jax.numpy as jnp
from jax import lax
from jax.experimental import pallas as pl
from jax.experimental.pallas import tpu as pltpu
from jax.sharding import PartitionSpec as P

MESH = pl.DeviceIdType.MESH
VMEM_LIMIT = 63 * 1024 * 1024
F32, BF16, I16 = jnp.float32, jnp.bfloat16, jnp.int16
AHEAD = 2
LAG = 5
RING = 3


def chunks_of(width):
    return max(n for n in range(1, 11) if width % (n * 128) == 0)


def tile_of(rows):
    return max(n for n in (256, 128, 64, 32, 16, 8) if rows % n == 0)


def greet(nn, nl, mn, ml):
    barrier = pltpu.get_barrier_semaphore()
    for k in range(1, nn):
        pl.semaphore_signal(barrier, inc=1, device_id={"node": lax.rem(mn + k, nn)}, device_id_type=MESH)
    for k in range(1, nl):
        pl.semaphore_signal(barrier, inc=1, device_id={"local": lax.rem(ml + k, nl)}, device_id_type=MESH)
    pl.semaphore_wait(barrier, nn + nl - 2)


def places(info, first, stride, count, topk):
    lines = info.shape[-1]
    expert = (lax.broadcasted_iota(jnp.int32, (count, lines), 0) * stride + first).astype(F32)
    named = jnp.zeros((count, lines), F32)
    weight = jnp.zeros((count, lines), F32)
    for k in range(topk):
        match = info[k : k + 1, :] == expert
        named = jnp.where(match, 1.0, named)
        weight = jnp.where(match, info[8 + k : 9 + k, :], weight)
    earlier = (
        lax.broadcasted_iota(jnp.int32, (lines, lines), 0) < lax.broadcasted_iota(jnp.int32, (lines, lines), 1)
    ).astype(F32)
    slot = jnp.dot(named, earlier, preferred_element_type=F32)
    return jnp.where(named > 0.0, slot, -1.0), weight


def chooser(info, first, stride, count, topk, cap):
    slot, _ = places(info, first, stride, count, topk)
    rank = lax.broadcasted_iota(jnp.int32, (cap, info.shape[-1]), 0).astype(F32)
    return jnp.concatenate(
        [jnp.where(slot[e : e + 1, :] == rank, 1.0, 0.0) for e in range(count)], axis=0
    ).astype(BF16)


def mixer(info, first, stride, count, topk, cap):
    slot, weight = places(info, first, stride, count, topk)
    rank = lax.broadcasted_iota(jnp.int32, (cap, info.shape[-1]), 0).astype(F32)
    back = jnp.concatenate(
        [jnp.where(slot[e : e + 1, :] == rank, weight[e : e + 1, :], 0.0) for e in range(count)], axis=0
    ).T
    high = back.astype(BF16)
    rest = back - high.astype(F32)
    middle = rest.astype(BF16)
    return jnp.concatenate([high, middle, (rest - middle.astype(F32)).astype(BF16)], axis=0)


def remote(src, dst, send, recv, **place):
    return pltpu.make_async_remote_copy(
        src_ref=src, dst_ref=dst, send_sem=send, recv_sem=recv, device_id=place, device_id_type=MESH
    )


def layer_kernel(
    nn, nl, nch, npl, cap, topk,
    tok, routes, gains, wg, wu, wd,
    out, loss,
    held, flat, sent, arrived, hid, dbuf, infos, peers, tallies, tally,
    got, got_scale, met, got_slim, got_thin,
    up_send, up_recv, dn_send, dn_recv, p_send, p_recv, g_send, g_recv, f_send, f_recv, v_send, v_recv,
    i_send, i_recv, j_send, j_recv, t_send, t_recv, own_sem, w_sem, d_sem,
    o_send, o_recv, z_send, z_recv, s_send, s_recv, V_send, V_recv, x_send, x_recv, q_send, q_recv, r_send, r_recv,
    free, free_up,
):
    mn, ml = lax.axis_index("node"), lax.axis_index("local")
    lines, width = tok.shape
    ch = width // nch
    nz = nch - npl
    ff = wg.shape[1]
    rows = nn * cap
    experts = nn * nl
    chips = max(nl // 2, 1)
    core = lax.rem(ml, 2)
    chip = ml // 2
    sibling = ml + 1 - 2 * core
    step = tile_of(nl * rows)
    wide = step // rows
    near, far = pl.ds(0, cap), pl.ds(cap, rows - cap)

    def cols(c):
        return pl.ds(pl.multiple_of(c * ch, 128), ch)

    def slots_of(e):
        return pl.ds(pl.multiple_of(e * cap, cap), cap)

    def chunk_at(t):
        return jnp.where(t == 0, 0, jnp.where(t <= npl, nz + t - 1, t - npl))

    def down_weights(t):
        slot = lax.rem(t, RING)
        return pltpu.make_async_copy(wd.at[:, cols(chunk_at(t))], dbuf.at[slot], d_sem.at[slot])

    def give(c, at, l, send, recv):
        k = lax.rem(l - ml + nl, nl)
        return remote(sent.at[c, l, at, :], arrived.at[c, ml, at, :], send.at[c, k - 1], recv.at[c, k - 1], local=l)

    def take(c, at, k, send, recv):
        e = lax.rem(ml + nl - k, nl)
        return remote(arrived.at[c, e, at, :], arrived.at[c, e, at, :], send.at[c, k - 1], recv.at[c, k - 1], local=e)

    def first_half(acc, wbuf, pick, choose):
        def weights(c):
            slot = lax.rem(c, RING)
            return (
                pltpu.make_async_copy(wg.at[cols(c), :], wbuf.at[slot, :, pl.ds(0, ff)], w_sem.at[slot, 0]),
                pltpu.make_async_copy(wu.at[cols(c), :], wbuf.at[slot, :, pl.ds(ff, ff)], w_sem.at[slot, 1]),
            )

        def own(c):
            return pltpu.make_async_copy(tok.at[:, cols(c)], held.at[c, mn], own_sem.at[c])

        def up(c, d, block):
            return remote(held.at[c, block], held.at[c, block], up_send.at[c, d], up_recv.at[c, d], node=mn + 1)

        def down(c, d, block):
            return remote(held.at[c, block], held.at[c, block], dn_send.at[c, d], dn_recv.at[c, d], node=mn - 1)

        def within(c, at, k):
            e = lax.rem(ml + k, nl)
            return remote(
                sent.at[c, e, at, :], arrived.at[c, ml, at, :], p_send.at[c, k - 1], p_recv.at[c, k - 1], local=e
            )

        def within_all(c, k):
            at = arrived.at[c, lax.rem(ml + nl - k, nl)]
            return remote(at, at, p_send.at[c, k - 1], p_recv.at[c, k - 1], local=lax.rem(ml + nl - k, nl))

        def own_flat(q):
            return pltpu.make_async_copy(tok.at[:, cols(nz + q)], flat.at[q, ml], own_sem.at[nz + q])

        def abroad(q, j):
            to = lax.rem(chip + j, chips) * 2 + core
            return remote(flat.at[q, ml], flat.at[q, ml], g_send.at[q, j - 1], g_recv.at[q, j - 1], local=to)

        def from_abroad(q, j):
            at = lax.rem(chip + chips - j, chips) * 2 + core
            return remote(flat.at[q, at], flat.at[q, at], g_send.at[q, j - 1], g_recv.at[q, j - 1], local=at)

        def across(q, j):
            at = lax.rem(chip + chips - j, chips) * 2 + core
            return remote(flat.at[q, at], flat.at[q, at], f_send.at[q, j], f_recv.at[q, j], local=sibling)

        def from_across(q, j):
            at = lax.rem(chip + chips - j, chips) * 2 + 1 - core
            return remote(flat.at[q, at], flat.at[q, at], f_send.at[q, j], f_recv.at[q, j], local=sibling)

        def upright(q, k):
            n = lax.rem(mn + k, nn)
            return remote(
                sent.at[nz + q, :, slots_of(n), :], arrived.at[nz + q, :, pl.ds((nn - k) * cap, cap), :],
                v_send.at[q, k - 1], v_recv.at[q, k - 1], node=n,
            )

        def info_copy(k):
            return remote(infos.at[mn], infos.at[mn], i_send.at[k - 1], i_recv.at[k - 1], node=lax.rem(mn + k, nn))

        def peer_copy(k):
            return remote(peers.at[ml], peers.at[ml], j_send.at[k - 1], j_recv.at[k - 1], local=lax.rem(ml + k, nl))

        def tally_copy(k):
            return remote(tally, tallies.at[ml], t_send.at[k - 1], t_recv.at[k - 1], local=lax.rem(ml + k, nl))

        def start_own(c):
            @pl.when(mn + 1 < nn)
            def _():
                up(c, 0, mn).start()

            @pl.when(mn > 0)
            def _():
                down(c, 0, mn).start()

        for q in range(npl):
            own_flat(q).start()

        @pl.loop(0, nz)
        def _(c):
            own(c).start()

        @pl.loop(0, min(RING, nch))
        def _(c):
            for copy in weights(c):
                copy.start()
            down_weights(c).start()

        mine = jnp.concatenate(
            [routes[...].astype(F32), jnp.zeros((8 - topk, lines), F32), gains[...], jnp.zeros((8 - topk, lines), F32)], axis=0
        )
        infos[mn] = mine
        peers[ml] = mine
        pick[mn] = chooser(mine, mn * nl, 1, nl, topk, cap)
        greet(nn, nl, mn, ml)

        for q in range(npl):
            own_flat(q).wait()
            for j in range(1, chips):
                abroad(q, j).start()
            across(q, 0).start()

        @pl.loop(0, AHEAD)
        def _(c):
            own(c).wait()
            start_own(c)

        for k in range(1, nn):
            info_copy(k).start()
        for k in range(1, nl):
            peer_copy(k).start()

        def choose_rows(c, j):
            n = lax.rem(mn + j, nn)
            rows_of = jnp.dot(pick[n], held[c, n], preferred_element_type=F32)
            sent[c, :, slots_of(j), :] = rows_of.reshape(nl, cap, ch).astype(BF16)

        def hand_out(c, at):
            for k in range(1, nl):
                within(c, at, k).start()
            arrived[c, ml, at, :] = sent[c, ml, at, :]

        @pl.loop(0, nz)
        def _(c):
            @pl.when(c >= AHEAD)
            def _():
                own(c).wait()

            choose_rows(c, 0)
            hand_out(c, near)

        for k in range(1, nn):
            info_copy(k).wait_recv()

        @pl.loop(0, nn)
        def _(n):
            @pl.when(n != mn)
            def _():
                pick[n] = chooser(infos[n], mn * nl, 1, nl, topk, cap)

        acc[...] = jnp.zeros(acc.shape, F32)

        def product(c, m):
            block = arrived[c, pl.ds(m * wide, wide)].reshape(step, ch)
            return jnp.dot(block, wbuf[lax.rem(c, RING)], preferred_element_type=F32)

        def multiply(c):
            for copy in weights(c):
                copy.wait()

            @pl.loop(0, nl // wide)
            def _(m):
                acc[pl.ds(pl.multiple_of(m * step, step), step), :] += product(c, m)

            @pl.when(c + RING < nch)
            def _():
                for copy in weights(c + RING):
                    copy.start()

        def hand_up(q):
            for j in range(chips):
                from_across(q, j).wait_recv()

            @pl.loop(0, nl)
            def _(l):
                sent[nz + q, l] = jnp.dot(choose[l], flat[q, l], preferred_element_type=F32).astype(BF16)
                arrived[nz + q, l, near, :] = sent[nz + q, l, slots_of(mn), :]

            for k in range(1, nn):
                upright(q, k).start()

        first_up = min(3, nz - 1)

        @pl.loop(0, nz + LAG)
        def _(i):
            @pl.when(i < nz)
            def _():
                @pl.when(i + AHEAD < nz)
                def _():
                    start_own(i + AHEAD)

                for d in range(nn - 1):
                    @pl.when(mn - 1 - d >= 0)
                    def _():
                        block = mn - 1 - d
                        up(i, d, block).wait_recv()

                        if d + 1 < nn - 1:
                            @pl.when(mn + 1 < nn)
                            def _():
                                up(i, d + 1, block).start()

                    @pl.when(mn + 1 + d < nn)
                    def _():
                        block = mn + 1 + d
                        down(i, d, block).wait_recv()

                        if d + 1 < nn - 1:
                            @pl.when(mn > 0)
                            def _():
                                down(i, d + 1, block).start()

                @pl.loop(1, nn)
                def _(j):
                    choose_rows(i, j)

                hand_out(i, far)

            if npl:
                @pl.when(i == 0)
                def _():
                    for k in range(1, nl):
                        peer_copy(k).wait_recv()

                    @pl.loop(0, nl)
                    def _(l):
                        choose[l] = chooser(peers[l], ml, nl, nn, topk, cap)

                @pl.when(i == min(1, nz - 1))
                def _():
                    for q in range(npl):
                        for j in range(1, chips):
                            from_abroad(q, j).wait_recv()
                            across(q, j).start()

                for q in range(npl):
                    @pl.when(i == (nz - 1 if q == npl - 1 else first_up + q))
                    def _():
                        hand_up(q)

            @pl.when((i >= LAG) & (i - LAG < nch - 1))
            def _():
                for k in range(1, nl):
                    within_all(i - LAG, k).wait_recv()
                multiply(i - LAG)

            @pl.when(i == 0)
            def _():
                label = lax.broadcasted_iota(jnp.int32, (tally.shape[1], lines), 0).astype(F32)
                hits = jnp.zeros(label.shape, F32)
                sums = jnp.zeros(label.shape, F32)
                for n in range(nn):
                    for k in range(topk):
                        match = infos[n, k : k + 1, :] == label
                        hits = hits + jnp.where(match, 1.0, 0.0)
                        sums = sums + jnp.where(match, infos[n, 8 + k : 9 + k, :], 0.0)
                line = lax.broadcasted_iota(jnp.int32, (8, tally.shape[1]), 0)
                both = jnp.where(
                    line == 0,
                    jnp.sum(hits.T, axis=0, keepdims=True),
                    jnp.where(line == 1, jnp.sum(sums.T, axis=0, keepdims=True), 0.0),
                )
                tally[...] = both
                tallies[ml] = both
                for k in range(1, nl):
                    tally_copy(k).start()

            @pl.when(i == nz - 1)
            def _():
                for k in range(1, nl):
                    tally_copy(k).wait_recv()
                total = tallies[0]
                for l in range(1, nl):
                    total = total + tallies[l]
                tokens = float(lines * experts)
                loss[...] = jnp.sum(total[0:1, :] * total[1:2, :], axis=1, keepdims=True) * (
                    experts / (topk * tokens * tokens)
                )

        last = nch - 1
        for k in range(1, nl):
            pl.semaphore_signal(free, inc=1, device_id={"local": lax.rem(ml + k, nl)}, device_id_type=MESH)

        if npl:
            @pl.loop(0, npl - 1)
            def _(q):
                for k in range(1, nn):
                    upright(q, k).wait_recv()
                multiply(nz + q)

            for k in range(1, nn):
                upright(npl - 1, k).wait_recv()
        else:
            for k in range(1, nl):
                within_all(last, k).wait_recv()
        for copy in weights(last):
            copy.wait()
        for k in range(1, nl):
            within_all(0, k).wait_send()
        down_weights(0).wait()
        pl.semaphore_wait(free, nl - 1)

        @pl.loop(0, nl // wide)
        def _(i):
            m = lax.rem(ml // wide + 1 + i, nl // wide)
            at = pl.ds(pl.multiple_of(m * step, step), step)
            both = acc[at, :] + product(last, m)
            gate = both[:, 0:ff]
            short = (gate / (1.0 + jnp.exp(-gate)) * both[:, ff : 2 * ff]).astype(BF16)
            hid[at, :] = short
            value = jnp.dot(short, dbuf[0], preferred_element_type=F32)
            sent[0, pl.ds(m * wide, wide)] = value.astype(BF16).reshape(wide, rows, ch)
            for u in range(wide):
                l = m * wide + u

                @pl.when(l != ml)
                def _():
                    give(0, far, l, p_send, p_recv).start()

                @pl.when(l == ml)
                def _():
                    arrived[0, ml] = sent[0, ml]

        for k in range(1, nn if npl else nl):
            to = {"node": lax.rem(mn + k, nn)} if npl else {"local": lax.rem(ml + k, nl)}
            pl.semaphore_signal(free_up, inc=1, device_id=to, device_id_type=MESH)

        @pl.when(RING < nch)
        def _():
            down_weights(RING).start()

        for k in range(1, nn):
            info_copy(k).wait_send()
        for k in range(1, nl):
            tally_copy(k).wait_send()
            peer_copy(k).wait_send()
            if not npl:
                peer_copy(k).wait_recv()
        for q in range(npl):
            across(q, 0).wait_send()
            for j in range(1, chips):
                abroad(q, j).wait_send()
                across(q, j).wait_send()
            for k in range(1, nn):
                upright(q, k).wait_send()

        @pl.loop(0, nz)
        def _(c):
            @pl.when(c > 0)
            def _():
                for k in range(1, nl):
                    within_all(c, k).wait_send()

            for d in range(nn - 1):
                @pl.when((mn + 1 < nn) & (mn - d >= 0))
                def _():
                    up(c, d, mn - d).wait_send()

                @pl.when((mn > 0) & (mn + d < nn))
                def _():
                    down(c, d, mn + d).wait_send()


    def second_half(mix, blur, work, part, scale, kept, lent, slim, thin):
        def along(c, p, toward):
            mine = jnp.where(p < mn, p, p - 1)
            there = jnp.where(p > mn, p, jnp.where(p == mn - 1, nn, p))
            return (
                remote(part.at[c, mine], got.at[c, there], z_send.at[c, mine], z_recv.at[c, there], node=mn + toward),
                remote(scale.at[c, mine], got_scale.at[c, there], s_send.at[c, mine], s_recv.at[c, there], node=mn + toward),
            )

        def land(c, slot, toward):
            for buffer, sem in ((got, z_recv), (got_scale, s_recv)):
                at = buffer.at[c, slot]
                remote(at, at, sem.at[c, slot], sem.at[c, slot], node=mn - toward).wait_recv()

        def ascend(q, k):
            n = lax.rem(mn + k, nn)
            return remote(
                sent.at[nz + q, :, pl.ds(k * cap, cap), :], arrived.at[nz + q, :, slots_of(mn), :], V_send.at[q, k - 1], V_recv.at[q, k - 1], node=n
            )

        def lend(q, j):
            return remote(lent.at[q, j], met.at[q, j], x_send.at[q, j], x_recv.at[q, j], local=sibling)

        def deal(q, j):
            to = lax.rem(chip + j, chips) * 2 + core
            return (
                remote(slim.at[q, j - 1], got_slim.at[q, j - 1], q_send.at[q, j - 1], q_recv.at[q, j - 1], local=to),
                remote(thin.at[q, j - 1], got_thin.at[q, j - 1], r_send.at[q, j - 1], r_recv.at[q, j - 1], local=to),
            )

        pl.semaphore_wait(free_up, (nn if npl else nl) - 1)

        @pl.loop(1, nch)
        def _(t):
            c = chunk_at(t)
            slot = lax.rem(t, RING)
            down_weights(t).wait()

            @pl.loop(0, nl // wide)
            def _(m):
                at = pl.ds(pl.multiple_of(m * step, step), step)
                value = jnp.dot(hid[at, :], dbuf[slot], preferred_element_type=F32)
                sent[c, pl.ds(m * wide, wide)] = value.astype(BF16).reshape(wide, rows, ch)

            @pl.when(t + RING < nch)
            def _():
                down_weights(t + RING).start()

            if npl:
                @pl.when(t <= npl)
                def _():
                    for k in range(1, nn):
                        ascend(t - 1, k).start()

                    @pl.loop(0, nl)
                    def _(l):
                        arrived[c, l, slots_of(mn), :] = sent[c, l, near, :]

            @pl.when(t > npl)
            def _():
                for k in range(1, nl):
                    give(c, far, lax.rem(ml + k, nl), p_send, p_recv).start()
                arrived[c, ml] = sent[c, ml]

        @pl.loop(0, nn)
        def _(n):
            mix[n] = mixer(infos[n], mn * nl, 1, nl, topk, cap)

        if npl:
            @pl.loop(0, nl)
            def _(l):
                blur[l] = mixer(peers[l], ml, nl, nn, topk, cap)

        diagonal = lax.broadcasted_iota(jnp.int32, (lines, lines), 0) == lax.broadcasted_iota(jnp.int32, (lines, lines), 1)

        def summed(terms):
            return terms[0:lines] + terms[lines : 2 * lines] + terms[2 * lines : 3 * lines]

        def blend(c, n):
            block = arrived[c, :, slots_of(lax.rem(n - mn + nn, nn)), :].reshape(nl * cap, ch)
            return summed(jnp.dot(mix[n], block, preferred_element_type=F32))

        def pack(value):
            peak = jnp.maximum(jnp.max(jnp.abs(value), axis=1, keepdims=True), 1e-30)
            short = jnp.round(value * (32767.0 / peak)).astype(jnp.int32).astype(I16)
            line = jnp.sum(jnp.where(diagonal, peak, 0.0), axis=0, keepdims=True)
            return short, jnp.broadcast_to(line, (8, lines))

        def unpack(short, line):
            peak = jnp.sum(jnp.where(diagonal, line[0:1, :], 0.0), axis=1, keepdims=True)
            return short.astype(jnp.int32).astype(F32) * (peak * (1.0 / 32767.0))

        def pass_on(c, p, toward, relay):
            work[...] = blend(c, p)

            @pl.when(relay)
            def _():
                land(c, p, toward)
                work[...] += unpack(got[c, p], got_scale[c, p])

            mine = jnp.where(p < mn, p, p - 1)
            part[c, mine], scale[c, mine] = pack(work[...])
            for copy in along(c, p, toward):
                copy.start()

        late = max(nz - 2, 0)

        @pl.loop(0, nz + nn - 2)
        def _(i):
            @pl.when(i < nz)
            def _():
                for k in range(1, nl):
                    take(i, far, k, p_send, p_recv).wait_recv()

            c_up = i - mn
            c_down = i - (nn - 1 - mn)
            for d in reversed(range(nn - 1)):
                @pl.when((c_up >= 0) & (c_up < nz) & (mn + 1 + d < nn))
                def _():
                    pass_on(c_up, mn + 1 + d, 1, mn > 0)

                @pl.when((c_down >= 0) & (c_down < nz) & (mn - 1 - d >= 0))
                def _():
                    pass_on(c_down, mn - 1 - d, -1, mn < nn - 1)

            @pl.when(i == late)
            def _():
                @pl.loop(0, nz)
                def _(c):
                    for k in range(1, nl):
                        give(c, near, lax.rem(ml + k, nl), o_send, o_recv).start()

            if npl:
                @pl.when(i == late)
                def _():
                    for q in range(npl):
                        for k in range(1, nn):
                            ascend(q, k).wait_recv()

                        @pl.loop(0, chips)
                        def _(j):
                            to = lax.rem(chip + j, chips) * 2
                            lent[q, j] = summed(
                                jnp.dot(blur[to + 1 - core], arrived[nz + q, to + 1 - core], preferred_element_type=F32)
                            )
                            lend(q, j).start()
                            kept[q, j] = summed(jnp.dot(blur[to + core], arrived[nz + q, to + core], preferred_element_type=F32))

                @pl.when(i == late + 1)
                def _():
                    for q in range(npl):
                        for j in range(chips):
                            lend(q, j).wait_recv()
                            if j:
                                slim[q, j - 1], thin[q, j - 1] = pack(kept[q, j] + met[q, j])
                                for copy in deal(q, j):
                                    copy.start()

        @pl.loop(0, nz)
        def _(c):
            for k in range(1, nl):
                take(c, near, k, o_send, o_recv).wait_recv()
            work[...] = blend(c, mn)

            @pl.when(mn > 0)
            def _():
                land(c, mn, 1)
                work[...] += unpack(got[c, mn], got_scale[c, mn])

            @pl.when(mn < nn - 1)
            def _():
                land(c, nn, -1)
                work[...] += unpack(got[c, nn], got_scale[c, nn])

            out[:, cols(c)] = work[...].astype(out.dtype)

        for q in range(npl):
            total = kept[q, 0] + met[q, 0]
            for j in range(1, chips):
                for copy in deal(q, j):
                    copy.wait_recv()
                total = total + unpack(got_slim[q, j - 1], got_thin[q, j - 1])
            out[:, cols(nz + q)] = total.astype(out.dtype)

        for q in range(npl):
            for k in range(1, nn):
                ascend(q, k).wait_send()
            for j in range(chips):
                lend(q, j).wait_send()
                if j:
                    for copy in deal(q, j):
                        copy.wait_send()

        @pl.loop(0, nz)
        def _(c):
            for k in range(1, nl):
                give(c, far, lax.rem(ml + k, nl), p_send, p_recv).wait_send()
                give(c, near, lax.rem(ml + k, nl), o_send, o_recv).wait_send()
            for d in range(nn - 1):
                @pl.when(mn + 1 + d < nn)
                def _():
                    for copy in along(c, mn + 1 + d, 1):
                        copy.wait_send()

                @pl.when(mn - 1 - d >= 0)
                def _():
                    for copy in along(c, mn - 1 - d, -1):
                        copy.wait_send()


    some, others = max(npl, 1), max(chips - 1, 1)
    pl.run_scoped(
        first_half,
        pltpu.VMEM((nl * rows, 2 * ff), F32),
        pltpu.VMEM((RING, ch, 2 * ff), BF16),
        pltpu.VMEM((nn, nl * cap, lines), BF16),
        pltpu.VMEM((nl, rows, lines), BF16),
    )
    pl.run_scoped(
        second_half,
        pltpu.VMEM((nn, 3 * lines, nl * cap), BF16),
        pltpu.VMEM((nl, 3 * lines, rows), BF16),
        pltpu.VMEM((lines, ch), F32),
        pltpu.VMEM((nz, nn - 1, lines, ch), I16),
        pltpu.VMEM((nz, nn - 1, 8, lines), F32),
        pltpu.VMEM((some, chips, lines, ch), F32),
        pltpu.VMEM((some, chips, lines, ch), F32),
        pltpu.VMEM((some, others, lines, ch), I16),
        pltpu.VMEM((some, others, 8, lines), F32),
    )


def sems(*shape):
    return pltpu.SemaphoreType.DMA(tuple(max(n, 1) for n in shape))


def local(tokens, routes, route_weights, w_gate, w_up, w_down):
    nn, nl = lax.axis_size("node"), lax.axis_size("local")
    exp_dev, width, ff = w_gate.shape
    experts = exp_dev * nn * nl
    assert exp_dev == 1
    lines, topk = routes.shape
    assert topk <= 8
    cap = 4 * lines * topk // (3 * experts)
    rows = nn * cap
    nch = chunks_of(width)
    ch = width // nch
    held_bytes = 2 * lines * width * 3 * nn + 4 * nl * rows * width
    npl = nch // 10 if nl % 2 == 0 and held_bytes <= VMEM_LIMIT * 3 // 4 else 0
    nz = nch - npl
    some = max(npl, 1)
    chips = max(nl // 2, 1)
    others = max(chips - 1, 1)
    spare = 1 if npl == 0 else nl
    wide = -(-experts // 128) * 128

    vmem = pl.BlockSpec(memory_space=pltpu.VMEM)
    hbm = pl.BlockSpec(memory_space=pl.ANY)
    mixed, loss = pl.pallas_call(
        functools.partial(layer_kernel, nn, nl, nch, npl, cap, topk),
        out_shape=(jax.ShapeDtypeStruct((lines, width), tokens.dtype), jax.ShapeDtypeStruct((1, 1), F32)),
        in_specs=[hbm, vmem, vmem, hbm, hbm, hbm],
        out_specs=(vmem, vmem),
        scratch_shapes=[
            pltpu.VMEM((nz, nn, lines, ch), BF16),
            pltpu.VMEM((some, spare, lines, ch), BF16),
            pltpu.VMEM((nch, nl, rows, ch), BF16),
            pltpu.VMEM((nch, nl, rows, ch), BF16),
            pltpu.VMEM((nl * rows, ff), BF16),
            pltpu.VMEM((RING, ff, ch), BF16),
            pltpu.VMEM((nn, 16, lines), F32),
            pltpu.VMEM((nl, 16, lines), F32),
            pltpu.VMEM((nl, 8, wide), F32),
            pltpu.VMEM((8, wide), F32),
            pltpu.VMEM((nz, nn + 1, lines, ch), I16),
            pltpu.VMEM((nz, nn + 1, 8, lines), F32),
            pltpu.VMEM((some, chips if npl else 1, lines, ch), F32),
            pltpu.VMEM((some, others if npl else 1, lines, ch), I16),
            pltpu.VMEM((some, others, 8, lines), F32),
            sems(nz, nn - 1), sems(nz, nn - 1), sems(nz, nn - 1), sems(nz, nn - 1),
            sems(nz, nl - 1), sems(nz, nl - 1),
            sems(some, chips - 1), sems(some, chips - 1), sems(some, chips), sems(some, chips),
            sems(some, nn - 1), sems(some, nn - 1),
            sems(nn - 1), sems(nn - 1), sems(nl - 1), sems(nl - 1), sems(nl - 1), sems(nl - 1),
            sems(nch), sems(RING, 2), sems(RING),
            sems(nz, nl - 1), sems(nz, nl - 1),
            sems(nz, nn - 1), sems(nz, nn + 1), sems(nz, nn - 1), sems(nz, nn + 1),
            sems(some, nn - 1), sems(some, nn - 1), sems(some, chips), sems(some, chips),
            sems(some, chips - 1), sems(some, chips - 1), sems(some, chips - 1), sems(some, chips - 1),
            pltpu.SemaphoreType.REGULAR, pltpu.SemaphoreType.REGULAR,
        ],
        compiler_params=pltpu.CompilerParams(collective_id=0, has_side_effects=True, vmem_limit_bytes=VMEM_LIMIT),
    )(tokens, routes.T, route_weights.T, w_gate[0], w_up[0], w_down[0])
    return (mixed, loss.reshape(()))


def solution(mesh):
    placed = (
        P(("node", "local"), None),
        P(("node", "local"), None),
        P(("node", "local"), None),
        P(("node", "local"), None, None),
        P(("node", "local"), None, None),
        P(("node", "local"), None, None),
    )
    return jax.shard_map(
        local,
        mesh=mesh,
        in_specs=placed,
        out_specs=(P(("node", "local"), None), P()),
        check_vma=False,
    )
```

time: 505 us -> 247 us (0.49)
  Pallas kernels: 397 us -> 238 us
  blocking collectives: 43.9 us -> 0 us
  matrix products: 34.2 us -> 0 us
  local copies, waits for them, and re-layouts: 11.3 us -> 2.46 us
  other arithmetic: 7.54 us -> 0 us
    pallas_call x2 -> x1, Pallas kernels: 397 us -> 238 us  [local(): pl.pallas_call(functools.partial(layer_kernel, nn, nl, nch, npl, cap, top...]
    all_gather x1 -> x0, blocking collectives: 43.9 us -> none  [local(): every = lax.all_gather(both, ('node', 'local'), axis=0, tiled=True)]
    dot_general x4 -> x0, matrix products: 34.2 us -> none  [the longest x1 12.4 us: local(): upper = jnp.dot(got, w_up[0], preferred_element_type=f32)]
    convert_element_type x3 -> x0, local copies, waits for them, and re-layouts: 7.44 us -> none  [the longest x2 7.44 us: local(): jnp.where(back[None], jnp.stack([high, middle, low])[..., None, None], 0.0)]
where the time goes in v3:
time: 247 us; the launch traced here: 242 us
  Pallas kernels  238 us (96%)
    pallas_call x1, Pallas kernels, local(): pl.pallas_call(functools.partial(layer_kernel, nn, nl, nch, npl, cap, top...  238 us

profile of v3, /device:TPU:0, one launch (start us, length us, event | category | flops | bytes accessed | tf_op | source)
XLA Modules:
  0.0 242.4 jit_solution(14055769981298393151)
XLA Ops:
  0.6 237.6 %shard_map.77 = (bf16[128,5120]{1,0:T(8,128)(2,1)}, f32[1,1]{1,0:T(1,128)}) custom-call(bf16[128,5120]{1,0:T(8,128)(2,1)} %tok.1, s32[6,128]{1,0:T(8,128)} %bitcast.9, f32[6,128]{1,0:T(8,128)} %bitcast.10, bf16[5120,768]{1,0:T(8,128)(2,1)} %bitcast.6, bf16[5120,768]{1,0:T(8,128)(2,1)} %bitcast.7, bf16[768,5120]{1,0:T(8,128)(2,1)} %bitcast.8), custom_call_target="tpu_custom_call" | custom-call | tf_op jit(solution)/shard_map/pallas_call | solution.py:731
  238.2 2.5 %copy.10 = bf16[128,5120]{1,0:T(8,128)(2,1)} copy(bf16[128,5120]{1,0:T(8,128)(2,1)} %get-tuple-element.8) | data formatting | bytes 2621440

commit v4 on v3

--- a/solution.py
+++ b/solution.py
@@ -29,7 +29,6 @@
         pl.semaphore_signal(barrier, inc=1, device_id={"node": lax.rem(mn + k, nn)}, device_id_type=MESH)
     for k in range(1, nl):
         pl.semaphore_signal(barrier, inc=1, device_id={"local": lax.rem(ml + k, nl)}, device_id_type=MESH)
-    pl.semaphore_wait(barrier, nn + nl - 2)
 
 
 def places(info, first, stride, count, topk):
@@ -83,7 +82,7 @@
     up_send, up_recv, dn_send, dn_recv, p_send, p_recv, g_send, g_recv, f_send, f_recv, v_send, v_recv,
     i_send, i_recv, j_send, j_recv, t_send, t_recv, own_sem, w_sem, d_sem,
     o_send, o_recv, z_send, z_recv, s_send, s_recv, V_send, V_recv, x_send, x_recv, q_send, q_recv, r_send, r_recv,
-    free, free_up,
+    free, free_up, free_last,
 ):
     mn, ml = lax.axis_index("node"), lax.axis_index("local")
     lines, width = tok.shape
@@ -122,8 +121,11 @@
         return remote(arrived.at[c, e, at, :], arrived.at[c, e, at, :], send.at[c, k - 1], recv.at[c, k - 1], local=e)
 
     def first_half(acc, wbuf, pick, choose):
-        def weights(c):
-            slot = lax.rem(c, RING)
+        def chunk_of(u):
+            return jnp.where(u < nz - 1, u, jnp.where(u < nch - 1, u + 1, nz - 1))
+
+        def weights(u):
+            slot, c = lax.rem(u, RING), chunk_of(u)
             return (
                 pltpu.make_async_copy(wg.at[cols(c), :], wbuf.at[slot, :, pl.ds(0, ff)], w_sem.at[slot, 0]),
                 pltpu.make_async_copy(wu.at[cols(c), :], wbuf.at[slot, :, pl.ds(ff, ff)], w_sem.at[slot, 1]),
@@ -192,6 +194,7 @@
             def _():
                 down(c, 0, mn).start()
 
+        greet(nn, nl, mn, ml)
         for q in range(npl):
             own_flat(q).start()
 
@@ -210,8 +213,7 @@
         )
         infos[mn] = mine
         peers[ml] = mine
-        pick[mn] = chooser(mine, mn * nl, 1, nl, topk, cap)
-        greet(nn, nl, mn, ml)
+        pl.semaphore_wait(pltpu.get_barrier_semaphore(), nn + nl - 2)
 
         for q in range(npl):
             own_flat(q).wait()
@@ -228,6 +230,7 @@
             info_copy(k).start()
         for k in range(1, nl):
             peer_copy(k).start()
+        pick[mn] = chooser(mine, mn * nl, 1, nl, topk, cap)
 
         def choose_rows(c, j):
             n = lax.rem(mn + j, nn)
@@ -259,21 +262,21 @@
 
         acc[...] = jnp.zeros(acc.shape, F32)
 
-        def product(c, m):
-            block = arrived[c, pl.ds(m * wide, wide)].reshape(step, ch)
-            return jnp.dot(block, wbuf[lax.rem(c, RING)], preferred_element_type=F32)
-
-        def multiply(c):
-            for copy in weights(c):
+        def product(u, m):
+            block = arrived[chunk_of(u), pl.ds(m * wide, wide)].reshape(step, ch)
+            return jnp.dot(block, wbuf[lax.rem(u, RING)], preferred_element_type=F32)
+
+        def multiply(u):
+            for copy in weights(u):
                 copy.wait()
 
             @pl.loop(0, nl // wide)
             def _(m):
-                acc[pl.ds(pl.multiple_of(m * step, step), step), :] += product(c, m)
-
-            @pl.when(c + RING < nch)
-            def _():
-                for copy in weights(c + RING):
+                acc[pl.ds(pl.multiple_of(m * step, step), step), :] += product(u, m)
+
+            @pl.when(u + RING < nch)
+            def _():
+                for copy in weights(u + RING):
                     copy.start()
 
         def hand_up(q):
@@ -347,7 +350,7 @@
                     def _():
                         hand_up(q)
 
-            @pl.when((i >= LAG) & (i - LAG < nch - 1))
+            @pl.when((i >= LAG) & (i - LAG < nz - 1))
             def _():
                 for k in range(1, nl):
                     within_all(i - LAG, k).wait_recv()
@@ -386,28 +389,27 @@
                     experts / (topk * tokens * tokens)
                 )
 
+        if npl:
+            @pl.loop(0, npl)
+            def _(q):
+                for k in range(1, nn):
+                    upright(q, k).wait_recv()
+                multiply(nz - 1 + q)
+
         last = nch - 1
         for k in range(1, nl):
             pl.semaphore_signal(free, inc=1, device_id={"local": lax.rem(ml + k, nl)}, device_id_type=MESH)
-
         if npl:
-            @pl.loop(0, npl - 1)
-            def _(q):
-                for k in range(1, nn):
-                    upright(q, k).wait_recv()
-                multiply(nz + q)
-
             for k in range(1, nn):
-                upright(npl - 1, k).wait_recv()
-        else:
-            for k in range(1, nl):
-                within_all(last, k).wait_recv()
+                pl.semaphore_signal(free_up, inc=1, device_id={"node": lax.rem(mn + k, nn)}, device_id_type=MESH)
         for copy in weights(last):
             copy.wait()
         for k in range(1, nl):
             within_all(0, k).wait_send()
         down_weights(0).wait()
         pl.semaphore_wait(free, nl - 1)
+        for k in range(1, nl):
+            within_all(nz - 1, k).wait_recv()
 
         @pl.loop(0, nl // wide)
         def _(i):
@@ -430,9 +432,8 @@
                 def _():
                     arrived[0, ml] = sent[0, ml]
 
-        for k in range(1, nn if npl else nl):
-            to = {"node": lax.rem(mn + k, nn)} if npl else {"local": lax.rem(ml + k, nl)}
-            pl.semaphore_signal(free_up, inc=1, device_id=to, device_id_type=MESH)
+        for k in range(1, nl):
+            pl.semaphore_signal(free_last, inc=1, device_id={"local": lax.rem(ml + k, nl)}, device_id_type=MESH)
 
         @pl.when(RING < nch)
         def _():
@@ -500,7 +501,8 @@
                 remote(thin.at[q, j - 1], got_thin.at[q, j - 1], r_send.at[q, j - 1], r_recv.at[q, j - 1], local=to),
             )
 
-        pl.semaphore_wait(free_up, (nn if npl else nl) - 1)
+        if npl:
+            pl.semaphore_wait(free_up, nn - 1)
 
         @pl.loop(1, nch)
         def _(t):
@@ -528,11 +530,20 @@
                     def _(l):
                         arrived[c, l, slots_of(mn), :] = sent[c, l, near, :]
 
+            @pl.when(t == nch - 1)
+            def _():
+                pl.semaphore_wait(free_last, nl - 1)
+
             @pl.when(t > npl)
             def _():
                 for k in range(1, nl):
                     give(c, far, lax.rem(ml + k, nl), p_send, p_recv).start()
                 arrived[c, ml] = sent[c, ml]
+
+        @pl.loop(0, nz)
+        def _(c):
+            for k in range(1, nl):
+                give(c, near, lax.rem(ml + k, nl), o_send, o_recv).start()
 
         @pl.loop(0, nn)
         def _(n):
@@ -594,13 +605,6 @@
                 @pl.when((c_down >= 0) & (c_down < nz) & (mn - 1 - d >= 0))
                 def _():
                     pass_on(c_down, mn - 1 - d, -1, mn < nn - 1)
-
-            @pl.when(i == late)
-            def _():
-                @pl.loop(0, nz)
-                def _(c):
-                    for k in range(1, nl):
-                        give(c, near, lax.rem(ml + k, nl), o_send, o_recv).start()
 
             if npl:
                 @pl.when(i == late)
@@ -759,7 +763,7 @@
             sems(nz, nn - 1), sems(nz, nn + 1), sems(nz, nn - 1), sems(nz, nn + 1),
             sems(some, nn - 1), sems(some, nn - 1), sems(some, chips), sems(some, chips),
             sems(some, chips - 1), sems(some, chips - 1), sems(some, chips - 1), sems(some, chips - 1),
-            pltpu.SemaphoreType.REGULAR, pltpu.SemaphoreType.REGULAR,
+            pltpu.SemaphoreType.REGULAR, pltpu.SemaphoreType.REGULAR, pltpu.SemaphoreType.REGULAR,
         ],
         compiler_params=pltpu.CompilerParams(collective_id=0, has_side_effects=True, vmem_limit_bytes=VMEM_LIMIT),
     )(tokens, routes.T, route_weights.T, w_gate[0], w_up[0], w_down[0])

time: 247 us -> 239 us (0.968); the launches traced: 242 us -> 239 us
  Pallas kernels: 238 us -> 234 us
    pallas_call x1, Pallas kernels: 238 us -> 234 us  [local(): pl.pallas_call(functools.partial(layer_kernel, nn, nl, nch, npl, cap, top...]
where the time goes in v4:
time: 239 us
  Pallas kernels  234 us (98%)
  local copies, waits for them, and re-layouts  2.46 us (1%)
  between operations  2.39 us (1%)
    pallas_call x1, Pallas kernels, local(): pl.pallas_call(functools.partial(layer_kernel, nn, nl, nch, npl, cap, top...  234 us

profile of v4, /device:TPU:0, one launch (start us, length us, event | category | flops | bytes accessed | tf_op | source)
XLA Modules:
  0.0 238.9 jit_solution(4962182026782168413)
XLA Ops:
  0.6 234.0 %shard_map.77 = (bf16[128,5120]{1,0:T(8,128)(2,1)}, f32[1,1]{1,0:T(1,128)}) custom-call(bf16[128,5120]{1,0:T(8,128)(2,1)} %tok.1, s32[6,128]{1,0:T(8,128)} %bitcast.9, f32[6,128]{1,0:T(8,128)} %bitcast.10, bf16[5120,768]{1,0:T(8,128)(2,1)} %bitcast.6, bf16[5120,768]{1,0:T(8,128)(2,1)} %bitcast.7, bf16[768,5120]{1,0:T(8,128)(2,1)} %bitcast.8), custom_call_target="tpu_custom_call" | custom-call | tf_op jit(solution)/shard_map/pallas_call | solution.py:735
  234.7 2.5 %copy.10 = bf16[128,5120]{1,0:T(8,128)(2,1)} copy(bf16[128,5120]{1,0:T(8,128)(2,1)} %get-tuple-element.8) | data formatting | bytes 2621440
